TPU v7x, 32 devices: a whole 2x2x4 slice. The times are simulated.
32 devices in a mesh: gx: 4 (over y, x), gy: 8 (over z, core).
Axes of the slice: x: 2, y: 2, z: 4, core: 2. Of those that a mesh axis runs over, the one named last changes fastest.
Arguments:
- sources: bfloat16 [1024, 64, 512], P(('gx', 'gy')), may hold values from -6 to 6
- projection: bfloat16 [512, 512], replicated, may hold values from -0.25 to 0.25
- translations: bfloat16 [5, 2, 512, 512], replicated, may hold values from -0.1875 to 0.1875
- angles: float32 [6, 1024, 256], P(None, ('gx', 'gy')), may hold values from -3.140625 to 3.140625
- interpolation: bfloat16 [256, 1024], replicated, may hold values from -0.25 to 0.25
- box_order: int32 [1024], P(('gx', 'gy')), may hold values from 0 to 1023, as said below
Outputs:
- targets: bfloat16 [1024, 128, 512], P(('gx', 'gy'))
Inputs may be any that keep to these rules, and one draw needn't show every extreme that they name: `box_order`: each aligned block of 32 entries (entries k * 32 to (k + 1) * 32 - 1) is a permutation of those same indices.
All inputs are finite; a program needn't handle non-finite values.
Results may differ from a plain program's by a relative error of at most 0.014.
Values may be sent and summed in bfloat16 or wider, within the bound.
A program may use at most 64 MiB of HBM per device.

v0:
```python
import functools

import jax
import jax.numpy as jnp
from jax import lax
from jax.experimental import pallas as pl
from jax.experimental.pallas import tpu as pltpu
from jax.sharding import PartitionSpec as P

SPLITS = 2


def level_plan(count_x, count_y):
    bits_x = count_x.bit_length() - 1
    bits_y = count_y.bit_length() - 1
    return [
        ("gy", bits_y - 1),
        ("gx", bits_x - 1),
        ("gy", bits_y - 2),
        ("gx", bits_x - 2),
        ("gy", bits_y - 3),
    ]


def kernel(
    count_x, count_y, per_peer, sides,
    inv_ref, src_ref, proj_ref, w_ref, cos0_ref, sin0_ref, ang_ref, interp_ref,
    out_ref,
    st0, got0, st1, got1, st2, got2, tmp_a, tmp_b, ang_got, cs, sn,
    a2a_send, a2a_recv, ang_send, ang_recv, ex_send, ex_recv,
):
    f32, bf16 = jnp.float32, jnp.bfloat16
    plan = level_plan(count_x, count_y)
    levels = len(plan)
    me_x = lax.axis_index("gx")
    me_y = lax.axis_index("gy")
    half = sides // SPLITS
    rows = 2 * half
    coeffs = st0.shape[-1]
    points = interp_ref.shape[1] // 2
    chunks = per_peer * SPLITS
    x_bits = [bit for axis, bit in plan if axis == "gx"]
    x_hbs = [(me_x // (1 << bit)) % 2 for bit in x_bits]
    partners = [me_x + (1 - 2 * hb) * (1 << bit) for hb, bit in zip(x_hbs, x_bits)]

    barrier = pltpu.get_barrier_semaphore()
    for k in range(1, count_y):
        pl.semaphore_signal(
            barrier, inc=1, device_id=(me_x, (me_y + k) % count_y),
            device_id_type=pl.DeviceIdType.MESH,
        )
    for partner in partners:
        pl.semaphore_signal(
            barrier, inc=1, device_id=(partner, me_y), device_id_type=pl.DeviceIdType.MESH
        )
    pl.semaphore_wait(barrier, count_y - 1 + len(partners))

    def ang_copy(k):
        peer = (me_y + k) % count_y
        return pltpu.make_async_remote_copy(
            src_ref=ang_ref.at[peer], dst_ref=ang_got.at[me_y],
            send_sem=ang_send.at[k], recv_sem=ang_recv.at[k],
            device_id=(me_x, peer), device_id_type=pl.DeviceIdType.MESH,
        )

    def a2a_copy(c, k):
        peer = (me_y + k) % count_y
        return pltpu.make_async_remote_copy(
            src_ref=st0.at[c, peer], dst_ref=got0.at[c, me_y],
            send_sem=a2a_send.at[c, k], recv_sem=a2a_recv.at[c, k],
            device_id=(me_x, peer), device_id_type=pl.DeviceIdType.MESH,
        )

    def swap_copy(which, c):
        source, target = ((st1, got1), (st2, got2))[which]
        return pltpu.make_async_remote_copy(
            src_ref=source.at[c], dst_ref=target.at[c],
            send_sem=ex_send.at[which, c], recv_sem=ex_recv.at[which, c],
            device_id=(partners[which], me_y), device_id_type=pl.DeviceIdType.MESH,
        )

    for k in range(1, count_y):
        ang_copy(k).start()
    ang_got[me_y] = ang_ref[me_y]

    def put(store, real, imag, cosine, sine):
        store(0, (cosine * real - sine * imag).astype(bf16))
        store(half, (sine * real + cosine * imag).astype(bf16))

    def project(c):
        r, q = c // SPLITS, c % SPLITS
        first = pl.multiple_of(q * half, half)
        group = jnp.concatenate(
            [src_ref[inv_ref[p * per_peer + r], pl.ds(first, half), :] for p in range(count_y)],
            axis=0,
        )
        prod = jnp.dot(group, proj_ref[...], preferred_element_type=f32)
        for p in range(count_y):
            block = prod[p * half : (p + 1) * half]

            def store(at, value, p=p):
                st0[c, p, at : at + half, :] = value

            slot = p * per_peer + r
            put(
                store, block[:, :coeffs], block[:, coeffs:],
                cos0_ref[pl.ds(slot, 1), :], sin0_ref[pl.ds(slot, 1), :],
            )

    def finish(prod, index, y, r, level, store):
        base = index * rows
        upper = prod[base : base + half]
        lower = prod[base + half : base + rows]
        real = upper[:, :coeffs] - lower[:, coeffs:]
        imag = lower[:, :coeffs] + upper[:, coeffs:]
        row = r * levels + level
        put(store, real, imag, cs[y, pl.ds(row, 1), :], sn[y, pl.ds(row, 1), :])

    def y_level(load, make_store, level, r):
        stride = 1 << plan[level][1]
        lows = [y for y in range(count_y) if (y // stride) % 2 == 0]
        low = jnp.concatenate([load(y) for y in lows], axis=0)
        high = jnp.concatenate([load(y + stride) for y in lows], axis=0)
        for h in range(2):
            prod = jnp.dot(low, w_ref[level, h, 0], preferred_element_type=f32)
            prod += jnp.dot(high, w_ref[level, h, 1], preferred_element_type=f32)
            for index, y in enumerate(lows):
                finish(prod, index, y + h * stride, r, level, make_store(y + h * stride))

    def x_level(mine, other, which, level, r, make_store):
        hb = x_hbs[which]
        prod = jnp.dot(mine, w_ref[level, hb, hb], preferred_element_type=f32)
        prod += jnp.dot(other, w_ref[level, hb, 1 - hb], preferred_element_type=f32)
        for y in range(count_y):
            finish(prod, y, y, r, level, make_store(y))

    def into(ref):
        def make_store(y):
            def store(at, value):
                ref[y, at : at + half, :] = value

            return store

        return make_store

    def into_chunk(ref, c):
        def make_store(y):
            def store(at, value):
                ref[c, y, at : at + half, :] = value

            return store

        return make_store

    def flat(value):
        return value.reshape(count_y * rows, coeffs)

    @pl.loop(0, chunks)
    def _(c):
        project(c)
        for k in range(1, count_y):
            a2a_copy(c, k).start()
        got0[c, me_y] = st0[c, me_y]

    for k in range(1, count_y):
        ang_copy(k).wait()
    for y in range(count_y):
        angle = ang_got[y]
        cs[y] = jnp.cos(angle)
        sn[y] = jnp.sin(angle)

    @pl.loop(0, chunks + 3)
    def _(t):
        @pl.when(t < chunks)
        def _():
            c = t
            for k in range(1, count_y):
                a2a_copy(c, k).wait()
            y_level(lambda y: got0[c, y], into_chunk(st1, c), 0, c // SPLITS)
            swap_copy(0, c).start()

        @pl.when((t >= 1) & (t < chunks + 1))
        def _():
            c = t - 1
            r = c // SPLITS
            swap_copy(0, c).wait()
            x_level(flat(st1[c]), flat(got1[c]), 0, 1, r, into(tmp_a))
            y_level(lambda y: tmp_a[y], into_chunk(st2, c), 2, r)
            swap_copy(1, c).start()

        @pl.when(t >= 3)
        def _():
            c = t - 3
            r, q = c // SPLITS, c % SPLITS
            swap_copy(1, c).wait()
            x_level(flat(st2[c]), flat(got2[c]), 1, 3, r, into(tmp_a))
            y_level(lambda y: tmp_a[y], into(tmp_b), 4, r)
            prod = jnp.dot(flat(tmp_b[...]), interp_ref[...], preferred_element_type=f32)
            first = pl.multiple_of(q * half, half)
            for y in range(count_y):
                upper = prod[y * rows : y * rows + half]
                lower = prod[y * rows + half : (y + 1) * rows]
                real = upper[:, :points] - lower[:, points:]
                imag = upper[:, points:] + lower[:, :points]
                out_ref[y * per_peer + r, pl.ds(first, half), :] = real.astype(bf16)
                out_ref[y * per_peer + r, pl.ds(first + sides, half), :] = imag.astype(bf16)


def local(sources, projection, translations, angles, interpolation, box_order):
    box_count, sides, points = sources.shape
    coeffs = projection.shape[1] // 2
    count_x, count_y = lax.axis_size("gx"), lax.axis_size("gy")
    per_peer = box_count // count_y
    levels = translations.shape[0]
    chunks = per_peer * SPLITS
    rows = 2 * sides // SPLITS
    slots = jnp.arange(box_count, dtype=jnp.int32)
    inverse = jnp.sum(
        jnp.where((box_order % box_count)[None, :] == slots[:, None], slots[None, :], 0), axis=1
    ).astype(jnp.int32)
    later = angles[1:].reshape(levels, count_y, per_peer, coeffs).transpose(1, 2, 0, 3)
    later = later.reshape(count_y, per_peer * levels, coeffs)
    weights = translations.reshape(levels, 2, 2, coeffs, 2 * coeffs)
    vmem = pl.BlockSpec(memory_space=pltpu.VMEM)
    state = pltpu.VMEM((chunks, count_y, rows, coeffs), jnp.bfloat16)
    single = pltpu.VMEM((count_y, rows, coeffs), jnp.bfloat16)
    phases = pltpu.VMEM((count_y, per_peer * levels, coeffs), jnp.float32)
    dma = pltpu.SemaphoreType.DMA
    return pl.pallas_call(
        functools.partial(kernel, count_x, count_y, per_peer, sides),
        out_shape=jax.ShapeDtypeStruct((box_count, 2 * sides, points), jnp.bfloat16),
        in_specs=[pl.BlockSpec(memory_space=pltpu.SMEM)] + [vmem] * 7,
        out_specs=vmem,
        scratch_shapes=[state] * 6 + [single] * 2 + [phases] * 3 + [
            dma((chunks, count_y)), dma((chunks, count_y)),
            dma((count_y,)), dma((count_y,)),
            dma((2, chunks)), dma((2, chunks)),
        ],
        compiler_params=pltpu.CompilerParams(
            collective_id=0, has_side_effects=True, vmem_limit_bytes=60 * 2**20
        ),
    )(
        inverse, sources, projection, weights, jnp.cos(angles[0]), jnp.sin(angles[0]),
        later, interpolation,
    )


def solution(mesh):
    placed = (
        P(("gx", "gy"), None, None),
        P(),
        P(),
        P(None, ("gx", "gy"), None),
        P(),
        P(("gx", "gy")),
    )
    return jax.shard_map(
        local, mesh=mesh, in_specs=placed, out_specs=P(("gx", "gy"), None, None), check_vma=False
    )
```

profile of v0, /device:TPU:0, one launch (start us, length us, event | category | flops | bytes accessed | tf_op | source)
XLA Modules:
  0.0 101.0 jit_solution(5874084626749009132)
XLA Ops:
  0.0 0.7 and_select_fusion
  0.7 0.6 select_reduce_fusion.inv_ref
  1.3 1.5 %sine_bitcast_fusion = (f32[32,256]{1,0:T(8,128)}, f32[32,256]{1,0:T(8,128)}) fusion(f32[6,32,256]{2,1,0:T(8,128)} %param.9), kind=kLoop, calls=%fused_computation | loop fusion | bytes 98304 | tf_op jit(solution)/shard_map/sin | solution.py:243
  2.8 0.9 slice.8
  3.8 0.7 copy.12.ang_ref
  4.6 91.8 %shard_map.64 = bf16[32,128,512]{2,1,0:T(8,128)(2,1)} custom-call(s32[32]{0:T(128)} %select_reduce_fusion.inv_ref, bf16[32,64,512]{2,1,0:T(8,128)(2,1)} %src_ref.1, bf16[512,512]{1,0:T(8,128)(2,1)} %proj_ref.1, bf16[5,2,2,256,512]{4,3,2,1,0:T(8,128)(2,1)} %bitcast.7, f32[32,256]{1,0:T(8,128)} %get-tuple-element.6.cos0_ref, ...), custom_call_target="tpu_custom_call" | custom-call | tf_op jit(solution)/shard_map/pallas_call | solution.py:229
  96.4 4.6 %copy.14 = bf16[32,128,512]{2,1,0:T(8,128)(2,1)} copy(bf16[32,128,512]{2,1,0:T(8,128)(2,1)} %shard_map.64) | data formatting | bytes 8388608
  (2 shorter events, 0.1 us)
where the time goes:
time: 101 us
  Pallas kernels  91.8 us (91%)
  local copies, waits for them, and re-layouts  7.9 us (8%)
  other arithmetic  1.28 us (1%)
    pallas_call x1, Pallas kernels, local(): pl.pallas_call(functools.partial(kernel, count_x, count_y, per_peer, side...  91.8 us
    unnamed x1, local copies, waits for them, and re-layouts  4.64 us

commit v1 on v0

v1 whole, which is shorter than its diff:
```python
import functools

import jax
import jax.numpy as jnp
from jax import lax
from jax.experimental import pallas as pl
from jax.experimental.pallas import tpu as pltpu
from jax.sharding import PartitionSpec as P

SIDES = 8
SIN = (1.0, -0.16666666666602138, 0.00833333096559207, -0.00019840860009446372,
       2.752520673490089e-06, -2.3888051249402636e-08)
COS = (1.0, -0.4999999999699515, 0.04166666647185967, -0.001388888415088631,
       2.480103815897482e-05, -2.752459905052806e-07, 1.9906439107985886e-09)


def level_plan(count_x, count_y):
    bits_x = count_x.bit_length() - 1
    bits_y = count_y.bit_length() - 1
    return [
        ("gy", bits_y - 1),
        ("gx", bits_x - 1),
        ("gy", bits_y - 2),
        ("gx", bits_x - 2),
        ("gy", bits_y - 3),
    ]


def cos_sin(angle):
    half = angle * 0.5
    square = half * half

    def poly(coefs):
        total = jnp.full_like(square, coefs[-1])
        for coef in coefs[-2::-1]:
            total = total * square + coef
        return total

    sine, cosine = half * poly(SIN), poly(COS)
    return 1.0 - 2.0 * (sine * sine), 2.0 * (sine * cosine)


def kernel(
    count_x, count_y, sides,
    order_ref, angles_hbm, src_hbm, proj_hbm, w_hbm, interp_hbm,
    out_ref,
    ang, src, proj, w, interp, inverse, c0, s0, sent, got, ping, pong, back, home,
    phase_out, phase_in, last_out, last_in, cs, sn, cs_last, sn_last,
    load_sem, in_send, in_recv, out_send, out_recv, ang_send, ang_recv,
):
    f32, bf16 = jnp.float32, jnp.bfloat16
    nx, ny = 4, 8
    boxes = src.shape[0]
    coeffs = proj.shape[1] // 2
    points = interp.shape[1] // 2
    per_peer = boxes // count_y
    xl, yl = count_x // nx, count_y // ny
    simple = xl == 1 and yl == 1
    chunks = sides // SIDES
    lanes = ang.shape[2] // 2
    me_x, me_y = lax.axis_index("gx"), lax.axis_index("gy")
    group, group_low = me_x // xl, me_x % xl
    mine = group * ny + me_y // yl

    def spot(j, i):
        p = (me_y + j) % count_y
        r = (me_x + i) % per_peer
        return group_low + xl * (r * yl + me_y % yl), p, p * per_peer + r

    def origin(k, m):
        x = group_low + xl * ((group + k) % nx)
        return x, group % yl + yl * ((me_y // yl + m) % ny)

    def onto(k):
        return (group + k) % nx

    def remote(j, i, act):
        if j or i % per_peer:
            if simple or j:
                act()
                return
        elif simple:
            return
        pl.when(spot(j, i)[0] != me_x)(act)

    barrier = pltpu.get_barrier_semaphore()
    expected = 0
    for k in range(nx):
        for m in range(ny):
            if simple and not (k or m):
                continue
            x, y = origin(k, m)
            if simple:
                pl.semaphore_signal(
                    barrier, inc=1, device_id=(x, y), device_id_type=pl.DeviceIdType.MESH
                )
            else:
                @pl.when((x != me_x) | (y != me_y))
                def _(x=x, y=y):
                    pl.semaphore_signal(
                        barrier, inc=1, device_id=(x, y), device_id_type=pl.DeviceIdType.MESH
                    )
    if simple:
        expected = nx * ny - 1
    else:
        for k in range(1, nx):
            pl.semaphore_signal(
                barrier, inc=1, device_id=(group_low + xl * onto(k), me_y),
                device_id_type=pl.DeviceIdType.MESH,
            )
        for m in range(1, count_y):
            pl.semaphore_signal(
                barrier, inc=1, device_id=(me_x, (me_y + m) % count_y),
                device_id_type=pl.DeviceIdType.MESH,
            )
        own = (me_x // xl % yl == me_y % yl).astype(jnp.int32)
        expected = nx * ny - own + nx - 1 + count_y - 1

    pairs = chunks // 2
    loads = [
        pltpu.make_async_copy(angles_hbm, ang, load_sem.at[0]),
        pltpu.make_async_copy(proj_hbm, proj, load_sem.at[1]),
        pltpu.make_async_copy(interp_hbm, interp, load_sem.at[2]),
        pltpu.make_async_copy(w_hbm, w, load_sem.at[3]),
    ]
    pieces = pltpu.make_async_copy(src_hbm, src, load_sem.at[4])
    loads[0].start()
    loads[1].start()
    pieces.start()
    loads[3].start()
    loads[2].start()

    local = order_ref[...] % boxes
    place = lax.broadcasted_iota(jnp.int32, local.shape, 1)
    for slot in range(boxes):
        inverse[slot] = jnp.max(jnp.where(local == slot, place, 0))

    loads[0].wait()
    for first in range(0, boxes, 8):
        for level in range(4):
            for part in range(2):
                phase_out[pl.ds(first * 8 + level * 2 + part, 8, stride=8), :] = ang[
                    level + 1, first : first + 8, part * lanes : (part + 1) * lanes
                ]
    for slot in range(boxes):
        for part in range(2):
            row = slot // per_peer * 8 + slot % per_peer * 2 + part
            last_out[row : row + 1, :] = ang[5, slot : slot + 1, part * lanes : (part + 1) * lanes]
    cosine, sine = cos_sin(ang[0])
    c0[...] = cosine
    s0[...] = sine

    def turn(real, imag, cosine, sine):
        return jnp.concatenate(
            [cosine * real - sine * imag, sine * real + cosine * imag], axis=0
        ).astype(bf16)

    def project(cc):
        first = pl.multiple_of(cc * 2 * SIDES, 2 * SIDES)
        for half in range(2):
            slots = range(half * boxes // 2, (half + 1) * boxes // 2)
            rows = jnp.concatenate(
                [src[inverse[slot], pl.ds(first, 2 * SIDES), :] for slot in slots], axis=0
            )
            prod = jnp.dot(rows, proj[...], preferred_element_type=f32)
            for index, slot in enumerate(slots):
                for part in range(2):
                    at = (index * 2 + part) * SIDES
                    block = prod[at : at + SIDES]
                    sent[cc * 2 + part, slot] = turn(
                        block[:, :coeffs], block[:, coeffs:],
                        c0[slot : slot + 1, :], s0[slot : slot + 1, :],
                    )

    def in_copy(c, j, i):
        x, y, slot = spot(j, i)
        return pltpu.make_async_remote_copy(
            src_ref=sent.at[c, slot], dst_ref=got.at[c, mine],
            send_sem=in_send.at[c], recv_sem=in_recv.at[c],
            device_id=(x, y), device_id_type=pl.DeviceIdType.MESH,
        )

    def phase_copy(j, i):
        x, y, slot = spot(j, i)
        return pltpu.make_async_remote_copy(
            src_ref=phase_out.at[pl.ds(pl.multiple_of(slot * 8, 8), 8), :],
            dst_ref=phase_in.at[pl.ds(pl.multiple_of(mine * 8, 8), 8), :],
            send_sem=ang_send.at[0], recv_sem=ang_recv.at[0],
            device_id=(x, y), device_id_type=pl.DeviceIdType.MESH,
        )

    def last_copy(j):
        p = (me_y + j) % count_y
        return pltpu.make_async_remote_copy(
            src_ref=last_out.at[pl.ds(pl.multiple_of(p * 8, 8), 8), :],
            dst_ref=last_in.at[pl.ds(pl.multiple_of(me_y * 8, 8), 8), :],
            send_sem=ang_send.at[1], recv_sem=ang_recv.at[1],
            device_id=(me_x, p), device_id_type=pl.DeviceIdType.MESH,
        )

    def out_copy(c, k):
        return pltpu.make_async_remote_copy(
            src_ref=back.at[c, onto(k)], dst_ref=home.at[c, group],
            send_sem=out_send.at[c], recv_sem=out_recv.at[c],
            device_id=(group_low + xl * onto(k), me_y), device_id_type=pl.DeviceIdType.MESH,
        )

    far = sorted(range(count_y), key=lambda j: -min(j, count_y - j))
    blocks = [(j, i) for j in far for i in range(per_peer)]

    def keep(copy_own):
        if simple:
            copy_own(spot(0, 0)[2])
        else:
            for i in range(per_peer):
                x, _, slot = spot(0, i)
                pl.when(x == me_x)(functools.partial(copy_own, slot))

    def settle(ref, sem, count):
        if simple:
            block = ref.at[pl.ds(0, count)]
            pltpu.make_async_copy(block, block, sem).wait()
        else:
            block = ref.at[pl.ds(0, count - own)]
            pltpu.make_async_copy(block, block, sem).wait()

    total = boxes - 1 if simple else boxes

    def send_chunk(c):
        for j, i in blocks:
            remote(j, i, lambda: in_copy(c, j, i).start())

        def copy_own(slot):
            got[c, mine] = sent[c, slot]

        keep(copy_own)

    loads[1].wait()
    pieces.wait()
    project(0)

    pl.semaphore_wait(barrier, expected)
    for j, i in blocks:
        remote(j, i, lambda: phase_copy(j, i).start())

    def own_phase(slot):
        phase_in[pl.ds(pl.multiple_of(mine * 8, 8), 8), :] = phase_out[
            pl.ds(pl.multiple_of(slot * 8, 8), 8), :
        ]

    keep(own_phase)
    send_chunk(0)
    for j in range(1, count_y):
        last_copy(j).start()
    here = pl.ds(pl.multiple_of(me_y * 8, 8), 8)
    last_in[here, :] = last_out[here, :]
    send_chunk(1)

    @pl.loop(1, pairs)
    def _(cc):
        project(cc)
        send_chunk(cc * 2)
        send_chunk(cc * 2 + 1)

    loads[2].wait()
    loads[3].wait()
    settle_rows = 8 * total if simple else 8 * (total - own)
    rows_seen = phase_in.at[pl.ds(0, settle_rows), :]
    pltpu.make_async_copy(rows_seen, rows_seen, ang_recv.at[0]).wait()
    cosine, sine = cos_sin(phase_in[...])
    cs[...] = cosine
    sn[...] = sine
    rows_seen = last_in.at[pl.ds(0, 8 * (count_y - 1)), :]
    pltpu.make_async_copy(rows_seen, rows_seen, ang_recv.at[1]).wait()
    cosine, sine = cos_sin(last_in[...])
    cs_last[...] = cosine
    sn_last[...] = sine

    def wide(ref, row):
        return jnp.concatenate([ref[row : row + 1, :], ref[row + 1 : row + 2, :]], axis=1)

    def level(load, store, number, stride, phase):
        lows = [b for b in range(nx * ny) if b // stride % 2 == 0]
        low = jnp.concatenate([load(b) for b in lows], axis=0)
        high = jnp.concatenate([load(b + stride) for b in lows], axis=0)
        for h in range(2):
            prod = jnp.dot(low, w[number, h, :coeffs, :], preferred_element_type=f32)
            prod += jnp.dot(high, w[number, h, coeffs:, :], preferred_element_type=f32)
            values = []
            for index, b in enumerate(lows):
                base = index * 2 * SIDES
                upper, lower = prod[base : base + SIDES], prod[base + SIDES : base + 2 * SIDES]
                real = upper[:, :coeffs] - lower[:, coeffs:]
                imag = lower[:, :coeffs] + upper[:, coeffs:]
                values.append((b + h * stride, turn(real, imag, *phase(b + h * stride))))
            store(values)

    def into(ref):
        def store(values):
            for b, value in values:
                ref[b] = value

        return store

    def phases(number):
        return lambda b: (wide(cs, b * 8 + number * 2), wide(sn, b * 8 + number * 2))

    def last_phases(b):
        g, yy = b // ny, b % ny
        row = (yy * yl + g % yl) * 8 + g // yl * 2
        return wide(cs_last, row), wide(sn_last, row)

    def middle(c):
        settle(got.at[c], in_recv.at[c], total)
        level(lambda b: got[c, b], into(ping), 0, 4, phases(0))
        level(lambda b: ping[b], into(pong), 1, 2 * ny, phases(1))
        level(lambda b: pong[b], into(ping), 2, 2, phases(2))

        def store(values):
            for b, value in values:
                back[c, b // ny, b % ny] = value

        level(lambda b: ping[b], store, 3, ny, phases(3))
        for k in range(1, nx):
            out_copy(c, k).start()
        home[c, group] = back[c, group]

    def final(c):
        seen = home.at[c, pl.ds(0, nx - 1)]
        pltpu.make_async_copy(seen, seen, out_recv.at[c]).wait()
        first = pl.multiple_of(c * SIDES, SIDES)

        def store(values):
            rows = jnp.concatenate([value for _, value in values], axis=0)
            prod = jnp.dot(rows, interp[...], preferred_element_type=f32)
            for index, (b, _) in enumerate(values):
                g, yy = b // ny, b % ny
                base = index * 2 * SIDES
                upper, lower = prod[base : base + SIDES], prod[base + SIDES : base + 2 * SIDES]
                real = upper[:, :points] - lower[:, points:]
                imag = upper[:, points:] + lower[:, :points]
                slot = (yy * yl + g % yl) * per_peer + g // yl
                out_ref[slot, pl.ds(first, SIDES), :] = real.astype(bf16)
                out_ref[slot, pl.ds(first + sides, SIDES), :] = imag.astype(bf16)

        level(lambda b: home[c, b // ny, b % ny], store, 4, 1, last_phases)

    middle(0)

    @pl.loop(1, chunks)
    def _(c):
        middle(c)
        final(c - 1)

    final(chunks - 1)

    for c in range(chunks):
        settle(sent.at[c], in_send.at[c], total)
        seen = back.at[c, pl.ds(0, nx - 1)]
        pltpu.make_async_copy(seen, seen, out_send.at[c]).wait()
    rows_seen = phase_out.at[pl.ds(0, settle_rows), :]
    pltpu.make_async_copy(rows_seen, rows_seen, ang_send.at[0]).wait()
    rows_seen = last_out.at[pl.ds(0, 8 * (count_y - 1)), :]
    pltpu.make_async_copy(rows_seen, rows_seen, ang_send.at[1]).wait()


def local(sources, projection, translations, angles, interpolation, box_order):
    boxes, sides, points = sources.shape
    coeffs = projection.shape[1] // 2
    count_x, count_y = lax.axis_size("gx"), lax.axis_size("gy")
    chunks = sides // SIDES
    f32, bf16 = jnp.float32, jnp.bfloat16
    anywhere = pl.BlockSpec(memory_space=pltpu.HBM)
    vmem = pl.BlockSpec(memory_space=pltpu.VMEM)
    state = pltpu.VMEM((chunks, boxes, 2 * SIDES, coeffs), bf16)
    one = pltpu.VMEM((boxes, 2 * SIDES, coeffs), bf16)
    grouped = pltpu.VMEM((chunks, 4, boxes // 4, 2 * SIDES, coeffs), bf16)
    phases = pltpu.VMEM((boxes * 8, coeffs // 2), f32)
    last = pltpu.VMEM((count_y * 8, coeffs // 2), f32)
    dma = pltpu.SemaphoreType.DMA
    return pl.pallas_call(
        functools.partial(kernel, count_x, count_y, sides),
        out_shape=jax.ShapeDtypeStruct((boxes, 2 * sides, points), bf16),
        in_specs=[vmem] + [anywhere] * 5,
        out_specs=vmem,
        scratch_shapes=[
            pltpu.VMEM(angles.shape, f32), pltpu.VMEM(sources.shape, bf16),
            pltpu.VMEM(projection.shape, bf16), pltpu.VMEM(translations.shape, bf16),
            pltpu.VMEM(interpolation.shape, bf16), pltpu.SMEM((boxes,), jnp.int32),
            pltpu.VMEM((boxes, coeffs), f32), pltpu.VMEM((boxes, coeffs), f32),
            state, state, one, one, grouped, grouped,
            phases, phases, last, last, phases, phases, last, last,
            dma((5,)), dma((chunks,)), dma((chunks,)), dma((chunks,)),
            dma((chunks,)), dma((2,)), dma((2,)),
        ],
        compiler_params=pltpu.CompilerParams(
            collective_id=0, has_side_effects=True, vmem_limit_bytes=60 * 2**20
        ),
    )(
        box_order.reshape(1, boxes), angles, sources, projection, translations, interpolation
    )


def solution(mesh):
    placed = (
        P(("gx", "gy"), None, None),
        P(),
        P(),
        P(None, ("gx", "gy"), None),
        P(),
        P(("gx", "gy")),
    )
    return jax.shard_map(
        local, mesh=mesh, in_specs=placed, out_specs=P(("gx", "gy"), None, None), check_vma=False
    )
```

time: 101 us -> 75.4 us (0.75)
  Pallas kernels: 91.8 us -> 70.6 us
  local copies, waits for them, and re-layouts: 7.9 us -> 4.64 us
  other arithmetic: 1.28 us -> 0 us
    pallas_call x1, Pallas kernels: 91.8 us -> 70.6 us  [local(): pl.pallas_call(functools.partial(kernel, count_x, count_y, sides), out_sh...]
    sin x1 -> x0, local copies, waits for them, and re-layouts: 1.52 us -> none  [local(): jnp.sin(angles[0])]
where the time goes in v1:
time: 75.4 us; the launch traced here: 75.2 us
  Pallas kernels  70.6 us (94%)
  local copies, waits for them, and re-layouts  4.64 us (6%)
    pallas_call x1, Pallas kernels, local(): pl.pallas_call(functools.partial(kernel, count_x, count_y, sides), out_sh...  70.6 us
    unnamed x1, local copies, waits for them, and re-layouts  4.64 us

profile of v1, /device:TPU:0, one launch (start us, length us, event | category | flops | bytes accessed | tf_op | source)
XLA Modules:
  0.0 75.2 jit_solution(4418700677531552071)
XLA Ops:
  0.0 70.6 %shard_map.64 = bf16[32,128,512]{2,1,0:T(8,128)(2,1)} custom-call(s32[1,32]{1,0:T(1,128)} %bitcast.1, f32[6,32,256]{2,1,0:T(8,128)} %angles_hbm.1, bf16[32,64,512]{2,1,0:T(8,128)(2,1)} %src_hbm.1, bf16[512,512]{1,0:T(8,128)(2,1)} %proj_hbm.1, bf16[5,2,512,512]{3,2,1,0:T(8,128)(2,1)} %w_hbm.1, bf16[256,1024]{1,0:T(8,128)(2,1)} %interp_hbm.1), custom_call_target="tpu_custom_call" | custom-call | tf_op jit(solution)/shard_map/pallas_call | solution.py:381
  70.6 4.6 %copy.8 = bf16[32,128,512]{2,1,0:T(8,128)(2,1)} copy(bf16[32,128,512]{2,1,0:T(8,128)(2,1)} %shard_map.64) | data formatting | bytes 8388608

commit v2 on v1

--- a/solution.py
+++ b/solution.py
@@ -8,6 +8,8 @@
 from jax.sharding import PartitionSpec as P
 
 SIDES = 8
+AHEAD = 2
+STEP = 3.140625 / 32766
 SIN = (1.0, -0.16666666666602138, 0.00833333096559207, -0.00019840860009446372,
        2.752520673490089e-06, -2.3888051249402636e-08)
 COS = (1.0, -0.4999999999699515, 0.04166666647185967, -0.001388888415088631,
@@ -40,12 +42,20 @@
     return 1.0 - 2.0 * (sine * sine), 2.0 * (sine * cosine)
 
 
+def code(angle):
+    return jnp.round(angle * (1 / STEP)).astype(jnp.int32).astype(jnp.int16)
+
+
+def decode(value):
+    return value.astype(jnp.int32).astype(jnp.float32) * STEP
+
+
 def kernel(
     count_x, count_y, sides,
     order_ref, angles_hbm, src_hbm, proj_hbm, w_hbm, interp_hbm,
     out_ref,
     ang, src, proj, w, interp, inverse, c0, s0, sent, got, ping, pong, back, home,
-    phase_out, phase_in, last_out, last_in, cs, sn, cs_last, sn_last,
+    staged, staged_last, phase_out, phase_in, last_out, last_in, cs, sn, cs_last, sn_last,
     load_sem, in_send, in_recv, out_send, out_recv, ang_send, ang_recv,
 ):
     f32, bf16 = jnp.float32, jnp.bfloat16
@@ -139,13 +149,19 @@
     for first in range(0, boxes, 8):
         for level in range(4):
             for part in range(2):
-                phase_out[pl.ds(first * 8 + level * 2 + part, 8, stride=8), :] = ang[
+                staged[pl.ds(first * 8 + level * 2 + part, 8, stride=8), :] = ang[
                     level + 1, first : first + 8, part * lanes : (part + 1) * lanes
                 ]
     for slot in range(boxes):
         for part in range(2):
             row = slot // per_peer * 8 + slot % per_peer * 2 + part
-            last_out[row : row + 1, :] = ang[5, slot : slot + 1, part * lanes : (part + 1) * lanes]
+            staged_last[row : row + 1, :] = ang[
+                5, slot : slot + 1, part * lanes : (part + 1) * lanes
+            ]
+    for slot in range(boxes):
+        phase_out[slot] = code(staged[slot * 8 : slot * 8 + 8, :])
+    for p in range(count_y):
+        last_out[p] = code(staged_last[p * 8 : p * 8 + 8, :])
     cosine, sine = cos_sin(ang[0])
     c0[...] = cosine
     s0[...] = sine
@@ -183,8 +199,7 @@
     def phase_copy(j, i):
         x, y, slot = spot(j, i)
         return pltpu.make_async_remote_copy(
-            src_ref=phase_out.at[pl.ds(pl.multiple_of(slot * 8, 8), 8), :],
-            dst_ref=phase_in.at[pl.ds(pl.multiple_of(mine * 8, 8), 8), :],
+            src_ref=phase_out.at[slot], dst_ref=phase_in.at[mine],
             send_sem=ang_send.at[0], recv_sem=ang_recv.at[0],
             device_id=(x, y), device_id_type=pl.DeviceIdType.MESH,
         )
@@ -192,8 +207,7 @@
     def last_copy(j):
         p = (me_y + j) % count_y
         return pltpu.make_async_remote_copy(
-            src_ref=last_out.at[pl.ds(pl.multiple_of(p * 8, 8), 8), :],
-            dst_ref=last_in.at[pl.ds(pl.multiple_of(me_y * 8, 8), 8), :],
+            src_ref=last_out.at[p], dst_ref=last_in.at[me_y],
             send_sem=ang_send.at[1], recv_sem=ang_recv.at[1],
             device_id=(me_x, p), device_id_type=pl.DeviceIdType.MESH,
         )
@@ -244,40 +258,35 @@
         remote(j, i, lambda: phase_copy(j, i).start())
 
     def own_phase(slot):
-        phase_in[pl.ds(pl.multiple_of(mine * 8, 8), 8), :] = phase_out[
-            pl.ds(pl.multiple_of(slot * 8, 8), 8), :
-        ]
+        phase_in[mine] = phase_out[slot]
 
     keep(own_phase)
     send_chunk(0)
     for j in range(1, count_y):
         last_copy(j).start()
-    here = pl.ds(pl.multiple_of(me_y * 8, 8), 8)
-    last_in[here, :] = last_out[here, :]
+    last_in[me_y] = last_out[me_y]
     send_chunk(1)
 
     @pl.loop(1, pairs)
     def _(cc):
         project(cc)
-        send_chunk(cc * 2)
-        send_chunk(cc * 2 + 1)
 
     loads[2].wait()
     loads[3].wait()
-    settle_rows = 8 * total if simple else 8 * (total - own)
-    rows_seen = phase_in.at[pl.ds(0, settle_rows), :]
-    pltpu.make_async_copy(rows_seen, rows_seen, ang_recv.at[0]).wait()
-    cosine, sine = cos_sin(phase_in[...])
+    settle(phase_in, ang_recv.at[0], total)
+    cosine, sine = cos_sin(decode(phase_in[...]))
     cs[...] = cosine
     sn[...] = sine
-    rows_seen = last_in.at[pl.ds(0, 8 * (count_y - 1)), :]
-    pltpu.make_async_copy(rows_seen, rows_seen, ang_recv.at[1]).wait()
-    cosine, sine = cos_sin(last_in[...])
+    seen = last_in.at[pl.ds(0, count_y - 1)]
+    pltpu.make_async_copy(seen, seen, ang_recv.at[1]).wait()
+    cosine, sine = cos_sin(decode(last_in[...]))
     cs_last[...] = cosine
     sn_last[...] = sine
 
-    def wide(ref, row):
-        return jnp.concatenate([ref[row : row + 1, :], ref[row + 1 : row + 2, :]], axis=1)
+    def wide(ref, block, row):
+        return jnp.concatenate(
+            [ref[block, row : row + 1, :], ref[block, row + 1 : row + 2, :]], axis=1
+        )
 
     def level(load, store, number, stride, phase):
         lows = [b for b in range(nx * ny) if b // stride % 2 == 0]
@@ -303,15 +312,20 @@
         return store
 
     def phases(number):
-        return lambda b: (wide(cs, b * 8 + number * 2), wide(sn, b * 8 + number * 2))
+        return lambda b: (wide(cs, b, number * 2), wide(sn, b, number * 2))
 
     def last_phases(b):
         g, yy = b // ny, b % ny
-        row = (yy * yl + g % yl) * 8 + g // yl * 2
-        return wide(cs_last, row), wide(sn_last, row)
+        y, row = yy * yl + g % yl, g // yl * 2
+        return wide(cs_last, y, row), wide(sn_last, y, row)
 
     def middle(c):
         settle(got.at[c], in_recv.at[c], total)
+
+        @pl.when(c + AHEAD < chunks)
+        def _():
+            send_chunk(c + AHEAD)
+
         level(lambda b: got[c, b], into(ping), 0, 4, phases(0))
         level(lambda b: ping[b], into(pong), 1, 2 * ny, phases(1))
         level(lambda b: pong[b], into(ping), 2, 2, phases(2))
@@ -358,10 +372,9 @@
         settle(sent.at[c], in_send.at[c], total)
         seen = back.at[c, pl.ds(0, nx - 1)]
         pltpu.make_async_copy(seen, seen, out_send.at[c]).wait()
-    rows_seen = phase_out.at[pl.ds(0, settle_rows), :]
-    pltpu.make_async_copy(rows_seen, rows_seen, ang_send.at[0]).wait()
-    rows_seen = last_out.at[pl.ds(0, 8 * (count_y - 1)), :]
-    pltpu.make_async_copy(rows_seen, rows_seen, ang_send.at[1]).wait()
+    settle(phase_out, ang_send.at[0], total)
+    seen = last_out.at[pl.ds(0, count_y - 1)]
+    pltpu.make_async_copy(seen, seen, ang_send.at[1]).wait()
 
 
 def local(sources, projection, translations, angles, interpolation, box_order):
@@ -375,12 +388,15 @@
     state = pltpu.VMEM((chunks, boxes, 2 * SIDES, coeffs), bf16)
     one = pltpu.VMEM((boxes, 2 * SIDES, coeffs), bf16)
     grouped = pltpu.VMEM((chunks, 4, boxes // 4, 2 * SIDES, coeffs), bf16)
-    phases = pltpu.VMEM((boxes * 8, coeffs // 2), f32)
-    last = pltpu.VMEM((count_y * 8, coeffs // 2), f32)
+    lanes = coeffs // 2
+    phases, last = pltpu.VMEM((boxes, 8, lanes), f32), pltpu.VMEM((count_y, 8, lanes), f32)
+    coded, coded_last = (
+        pltpu.VMEM((boxes, 8, lanes), jnp.int16), pltpu.VMEM((count_y, 8, lanes), jnp.int16)
+    )
     dma = pltpu.SemaphoreType.DMA
     return pl.pallas_call(
         functools.partial(kernel, count_x, count_y, sides),
-        out_shape=jax.ShapeDtypeStruct((boxes, 2 * sides, points), bf16),
+        out_shape=pltpu.VMEM((boxes, 2 * sides, points), bf16),
         in_specs=[vmem] + [anywhere] * 5,
         out_specs=vmem,
         scratch_shapes=[
@@ -389,15 +405,22 @@
             pltpu.VMEM(interpolation.shape, bf16), pltpu.SMEM((boxes,), jnp.int32),
             pltpu.VMEM((boxes, coeffs), f32), pltpu.VMEM((boxes, coeffs), f32),
             state, state, one, one, grouped, grouped,
-            phases, phases, last, last, phases, phases, last, last,
+            pltpu.VMEM((boxes * 8, lanes), f32), pltpu.VMEM((count_y * 8, lanes), f32),
+            coded, coded, coded_last, coded_last, phases, phases, last, last,
             dma((5,)), dma((chunks,)), dma((chunks,)), dma((chunks,)),
             dma((chunks,)), dma((2,)), dma((2,)),
         ],
         compiler_params=pltpu.CompilerParams(
-            collective_id=0, has_side_effects=True, vmem_limit_bytes=60 * 2**20
+            collective_id=0, has_side_effects=True, vmem_limit_bytes=40 * 2**20
         ),
     )(
-        box_order.reshape(1, boxes), angles, sources, projection, translations, interpolation
+        *[
+            pltpu.with_memory_space_constraint(value, pltpu.HBM)
+            for value in (
+                box_order.reshape(1, boxes), angles, sources, projection, translations,
+                interpolation,
+            )
+        ]
     )
 
 

time: 75.4 us -> 66.4 us (0.88)
  Pallas kernels: 70.6 us -> 64.2 us
  local copies, waits for them, and re-layouts: 4.64 us -> 2.02 us
    pallas_call x1, Pallas kernels: 70.6 us -> 64.2 us  [local(): pl.pallas_call(functools.partial(kernel, count_x, count_y, sides), out_sh...]
    unnamed x1, local copies, waits for them, and re-layouts: 4.64 us -> 2.02 us
where the time goes in v2:
time: 66.4 us; the launch traced here: 66.2 us
  Pallas kernels  64.2 us (97%)
  local copies, waits for them, and re-layouts  2.02 us (3%)
    pallas_call x1, Pallas kernels, local(): pl.pallas_call(functools.partial(kernel, count_x, count_y, sides), out_sh...  64.2 us
    unnamed x1, local copies, waits for them, and re-layouts  2.02 us

profile of v2, /device:TPU:0, one launch (start us, length us, event | category | flops | bytes accessed | tf_op | source)
XLA Modules:
  0.0 66.2 jit_solution(10564492776474153056)
XLA Ops:
  0.0 64.2 %shard_map.64 = bf16[32,128,512]{2,1,0:T(8,128)(2,1)S(1)} custom-call(s32[1,32]{1,0:T(1,128)} %bitcast.1, f32[6,32,256]{2,1,0:T(8,128)} %angles_hbm.1, bf16[32,64,512]{2,1,0:T(8,128)(2,1)} %src_hbm.1, bf16[512,512]{1,0:T(8,128)(2,1)} %proj_hbm.1, bf16[5,2,512,512]{3,2,1,0:T(8,128)(2,1)} %w_hbm.1, bf16[256,1024]{1,0:T(8,128)(2,1)} %interp_hbm.1), custom_call_target="tpu_custom_call" | custom-call | tf_op jit(solution)/shard_map/pallas_call | solution.py:397
  64.2 2.0 %copy.8 = bf16[32,128,512]{2,1,0:T(8,128)(2,1)} copy(bf16[32,128,512]{2,1,0:T(8,128)(2,1)S(1)} %shard_map.64) | data formatting | bytes 8388608

commit v3 on v2

--- a/solution.py
+++ b/solution.py
@@ -56,7 +56,7 @@
     out_ref,
     ang, src, proj, w, interp, inverse, c0, s0, sent, got, ping, pong, back, home,
     staged, staged_last, phase_out, phase_in, last_out, last_in, cs, sn, cs_last, sn_last,
-    load_sem, in_send, in_recv, out_send, out_recv, ang_send, ang_recv,
+    ready, load_sem, in_send, in_recv, out_send, out_recv, ang_send, ang_recv,
 ):
     f32, bf16 = jnp.float32, jnp.bfloat16
     nx, ny = 4, 8
@@ -97,7 +97,7 @@
     expected = 0
     for k in range(nx):
         for m in range(ny):
-            if simple and not (k or m):
+            if simple and (k == 0) == (m == 0):
                 continue
             x, y = origin(k, m)
             if simple:
@@ -111,7 +111,7 @@
                         barrier, inc=1, device_id=(x, y), device_id_type=pl.DeviceIdType.MESH
                     )
     if simple:
-        expected = nx * ny - 1
+        expected = nx - 1 + ny - 1
     else:
         for k in range(1, nx):
             pl.semaphore_signal(
@@ -212,10 +212,10 @@
             device_id=(me_x, p), device_id_type=pl.DeviceIdType.MESH,
         )
 
-    def out_copy(c, k):
+    def out_copy(c, odd, k):
         return pltpu.make_async_remote_copy(
-            src_ref=back.at[c, onto(k)], dst_ref=home.at[c, group],
-            send_sem=out_send.at[c], recv_sem=out_recv.at[c],
+            src_ref=back.at[c, odd, onto(k)], dst_ref=home.at[c, odd, group],
+            send_sem=out_send.at[c, odd], recv_sem=out_recv.at[c, odd],
             device_id=(group_low + xl * onto(k), me_y), device_id_type=pl.DeviceIdType.MESH,
         )
 
@@ -240,32 +240,52 @@
 
     total = boxes - 1 if simple else boxes
 
-    def send_chunk(c):
-        for j, i in blocks:
+    def send_part(c, part):
+        for j, i in part:
             remote(j, i, lambda: in_copy(c, j, i).start())
 
+    def keep_chunk(c):
         def copy_own(slot):
             got[c, mine] = sent[c, slot]
 
         keep(copy_own)
+
+    def send_chunk(c):
+        send_part(c, blocks)
+        keep_chunk(c)
 
     loads[1].wait()
     pieces.wait()
     project(0)
 
+    near = [(j, i) for j, i in blocks if j == 0 or i == 0] if simple else blocks
+    others = [(j, i) for j, i in blocks if j and i] if simple else []
     pl.semaphore_wait(barrier, expected)
-    for j, i in blocks:
+    if simple:
+        for k in range(1, nx):
+            pl.semaphore_signal(
+                ready, inc=1, device_id=(onto(k), me_y), device_id_type=pl.DeviceIdType.MESH
+            )
+    for j, i in near:
         remote(j, i, lambda: phase_copy(j, i).start())
+    send_part(0, near)
+    for j in range(1, count_y):
+        last_copy(j).start()
+    send_part(1, near)
 
     def own_phase(slot):
         phase_in[mine] = phase_out[slot]
 
     keep(own_phase)
-    send_chunk(0)
-    for j in range(1, count_y):
-        last_copy(j).start()
     last_in[me_y] = last_out[me_y]
-    send_chunk(1)
+    keep_chunk(0)
+    keep_chunk(1)
+    if simple:
+        pl.semaphore_wait(ready, nx - 1)
+    for j, i in others:
+        remote(j, i, lambda: phase_copy(j, i).start())
+    send_part(0, others)
+    send_part(1, others)
 
     @pl.loop(1, pairs)
     def _(cc):
@@ -288,8 +308,8 @@
             [ref[block, row : row + 1, :], ref[block, row + 1 : row + 2, :]], axis=1
         )
 
-    def level(load, store, number, stride, phase):
-        lows = [b for b in range(nx * ny) if b // stride % 2 == 0]
+    def level(load, store, number, stride, phase, odd=(0, 1)):
+        lows = [b for b in range(nx * ny) if b // stride % 2 == 0 and b % 2 in odd]
         low = jnp.concatenate([load(b) for b in lows], axis=0)
         high = jnp.concatenate([load(b + stride) for b in lows], axis=0)
         for h in range(2):
@@ -326,22 +346,24 @@
         def _():
             send_chunk(c + AHEAD)
 
-        level(lambda b: got[c, b], into(ping), 0, 4, phases(0))
-        level(lambda b: ping[b], into(pong), 1, 2 * ny, phases(1))
-        level(lambda b: pong[b], into(ping), 2, 2, phases(2))
 
         def store(values):
             for b, value in values:
-                back[c, b // ny, b % ny] = value
-
-        level(lambda b: ping[b], store, 3, ny, phases(3))
-        for k in range(1, nx):
-            out_copy(c, k).start()
-        home[c, group] = back[c, group]
+                back[c, b % 2, b // ny, b % ny // 2] = value
+
+        for odd in range(2):
+            level(lambda b: got[c, b], into(ping), 0, 4, phases(0), (odd,))
+            level(lambda b: ping[b], into(pong), 1, 2 * ny, phases(1), (odd,))
+            level(lambda b: pong[b], into(ping), 2, 2, phases(2), (odd,))
+            level(lambda b: ping[b], store, 3, ny, phases(3), (odd,))
+            for k in range(1, nx):
+                out_copy(c, odd, k).start()
+            home[c, odd, group] = back[c, odd, group]
 
     def final(c):
-        seen = home.at[c, pl.ds(0, nx - 1)]
-        pltpu.make_async_copy(seen, seen, out_recv.at[c]).wait()
+        for odd in range(2):
+            seen = home.at[c, odd, pl.ds(0, nx - 1)]
+            pltpu.make_async_copy(seen, seen, out_recv.at[c, odd]).wait()
         first = pl.multiple_of(c * SIDES, SIDES)
 
         def store(values):
@@ -357,7 +379,7 @@
                 out_ref[slot, pl.ds(first, SIDES), :] = real.astype(bf16)
                 out_ref[slot, pl.ds(first + sides, SIDES), :] = imag.astype(bf16)
 
-        level(lambda b: home[c, b // ny, b % ny], store, 4, 1, last_phases)
+        level(lambda b: home[c, b % 2, b // ny, b % ny // 2], store, 4, 1, last_phases)
 
     middle(0)
 
@@ -366,15 +388,16 @@
         middle(c)
         final(c - 1)
 
-    final(chunks - 1)
-
     for c in range(chunks):
         settle(sent.at[c], in_send.at[c], total)
-        seen = back.at[c, pl.ds(0, nx - 1)]
-        pltpu.make_async_copy(seen, seen, out_send.at[c]).wait()
+        for odd in range(2):
+            seen = back.at[c, odd, pl.ds(0, nx - 1)]
+            pltpu.make_async_copy(seen, seen, out_send.at[c, odd]).wait()
     settle(phase_out, ang_send.at[0], total)
     seen = last_out.at[pl.ds(0, count_y - 1)]
     pltpu.make_async_copy(seen, seen, ang_send.at[1]).wait()
+
+    final(chunks - 1)
 
 
 def local(sources, projection, translations, angles, interpolation, box_order):
@@ -387,7 +410,7 @@
     vmem = pl.BlockSpec(memory_space=pltpu.VMEM)
     state = pltpu.VMEM((chunks, boxes, 2 * SIDES, coeffs), bf16)
     one = pltpu.VMEM((boxes, 2 * SIDES, coeffs), bf16)
-    grouped = pltpu.VMEM((chunks, 4, boxes // 4, 2 * SIDES, coeffs), bf16)
+    grouped = pltpu.VMEM((chunks, 2, 4, boxes // 8, 2 * SIDES, coeffs), bf16)
     lanes = coeffs // 2
     phases, last = pltpu.VMEM((boxes, 8, lanes), f32), pltpu.VMEM((count_y, 8, lanes), f32)
     coded, coded_last = (
@@ -407,8 +430,8 @@
             state, state, one, one, grouped, grouped,
             pltpu.VMEM((boxes * 8, lanes), f32), pltpu.VMEM((count_y * 8, lanes), f32),
             coded, coded, coded_last, coded_last, phases, phases, last, last,
-            dma((5,)), dma((chunks,)), dma((chunks,)), dma((chunks,)),
-            dma((chunks,)), dma((2,)), dma((2,)),
+            pltpu.SemaphoreType.REGULAR, dma((5,)), dma((chunks,)), dma((chunks,)), dma((chunks, 2)),
+            dma((chunks, 2)), dma((2,)), dma((2,)),
         ],
         compiler_params=pltpu.CompilerParams(
             collective_id=0, has_side_effects=True, vmem_limit_bytes=40 * 2**20

time: 66.4 us -> 65.6 us (0.988)
  Pallas kernels: 64.2 us -> 63.4 us
    pallas_call x1, Pallas kernels: 64.2 us -> 63.4 us  [local(): pl.pallas_call(functools.partial(kernel, count_x, count_y, sides), out_sh...]
where the time goes in v3:
time: 65.6 us; the launch traced here: 65.5 us
  Pallas kernels  63.4 us (97%)
  local copies, waits for them, and re-layouts  2.02 us (3%)
    pallas_call x1, Pallas kernels, local(): pl.pallas_call(functools.partial(kernel, count_x, count_y, sides), out_sh...  63.4 us
    unnamed x1, local copies, waits for them, and re-layouts  2.02 us

profile of v3, /device:TPU:0, one launch (start us, length us, event | category | flops | bytes accessed | tf_op | source)
XLA Modules:
  0.0 65.5 jit_solution(11680670814661071661)
XLA Ops:
  0.0 63.4 %shard_map.64 = bf16[32,128,512]{2,1,0:T(8,128)(2,1)S(1)} custom-call(s32[1,32]{1,0:T(1,128)} %bitcast.1, f32[6,32,256]{2,1,0:T(8,128)} %angles_hbm.1, bf16[32,64,512]{2,1,0:T(8,128)(2,1)} %src_hbm.1, bf16[512,512]{1,0:T(8,128)(2,1)} %proj_hbm.1, bf16[5,2,512,512]{3,2,1,0:T(8,128)(2,1)} %w_hbm.1, bf16[256,1024]{1,0:T(8,128)(2,1)} %interp_hbm.1), custom_call_target="tpu_custom_call" | custom-call | tf_op jit(solution)/shard_map/pallas_call | solution.py:420
  63.4 2.0 %copy.8 = bf16[32,128,512]{2,1,0:T(8,128)(2,1)} copy(bf16[32,128,512]{2,1,0:T(8,128)(2,1)S(1)} %shard_map.64) | data formatting | bytes 8388608

commit v4 on v3

--- a/solution.py
+++ b/solution.py
@@ -73,7 +73,7 @@
     mine = group * ny + me_y // yl
 
     def spot(j, i):
-        p = (me_y + j) % count_y
+        p = (me_y // 2 + j // 2) % (count_y // 2) * 2 + (me_y + j) % 2
         r = (me_x + i) % per_peer
         return group_low + xl * (r * yl + me_y % yl), p, p * per_peer + r
 
@@ -219,8 +219,10 @@
             device_id=(group_low + xl * onto(k), me_y), device_id_type=pl.DeviceIdType.MESH,
         )
 
-    far = sorted(range(count_y), key=lambda j: -min(j, count_y - j))
+    far = sorted(range(count_y), key=lambda j: -min(j // 2, count_y // 2 - j // 2))
     blocks = [(j, i) for j in far for i in range(per_peer)]
+    early = [(j, i) for j, i in blocks if j < 2]
+    late = [(j, i) for j, i in blocks if j >= 2]
 
     def keep(copy_own):
         if simple:
@@ -251,8 +253,7 @@
         keep(copy_own)
 
     def send_chunk(c):
-        send_part(c, blocks)
-        keep_chunk(c)
+        send_part(c, late)
 
     loads[1].wait()
     pieces.wait()
@@ -290,6 +291,9 @@
     @pl.loop(1, pairs)
     def _(cc):
         project(cc)
+        for c in (cc * 2, cc * 2 + 1):
+            send_part(c, early)
+            keep_chunk(c)
 
     loads[2].wait()
     loads[3].wait()
@@ -381,23 +385,26 @@
 
         level(lambda b: home[c, b % 2, b // ny, b % ny // 2], store, 4, 1, last_phases)
 
-    middle(0)
-
-    @pl.loop(1, chunks)
-    def _(c):
-        middle(c)
-        final(c - 1)
-
-    for c in range(chunks):
-        settle(sent.at[c], in_send.at[c], total)
-        for odd in range(2):
-            seen = back.at[c, odd, pl.ds(0, nx - 1)]
-            pltpu.make_async_copy(seen, seen, out_send.at[c, odd]).wait()
-    settle(phase_out, ang_send.at[0], total)
-    seen = last_out.at[pl.ds(0, count_y - 1)]
-    pltpu.make_async_copy(seen, seen, ang_send.at[1]).wait()
-
-    final(chunks - 1)
+    @pl.loop(0, chunks + 1)
+    def _(t):
+        @pl.when(t < chunks)
+        def _():
+            middle(t)
+
+        @pl.when(t == chunks)
+        def _():
+            for c in range(chunks):
+                settle(sent.at[c], in_send.at[c], total)
+                for odd in range(2):
+                    seen = back.at[c, odd, pl.ds(0, nx - 1)]
+                    pltpu.make_async_copy(seen, seen, out_send.at[c, odd]).wait()
+            settle(phase_out, ang_send.at[0], total)
+            seen = last_out.at[pl.ds(0, count_y - 1)]
+            pltpu.make_async_copy(seen, seen, ang_send.at[1]).wait()
+
+        @pl.when(t >= 1)
+        def _():
+            final(t - 1)
 
 
 def local(sources, projection, translations, angles, interpolation, box_order):

time: 65.6 us -> 64.9 us (0.989)
  Pallas kernels: 63.4 us -> 62.7 us
    pallas_call x1, Pallas kernels: 63.4 us -> 62.7 us  [local(): pl.pallas_call(functools.partial(kernel, count_x, count_y, sides), out_sh...]
where the time goes in v4:
time: 64.9 us; the launch traced here: 64.7 us
  Pallas kernels  62.7 us (97%)
  local copies, waits for them, and re-layouts  2.02 us (3%)
    pallas_call x1, Pallas kernels, local(): pl.pallas_call(functools.partial(kernel, count_x, count_y, sides), out_sh...  62.7 us
    unnamed x1, local copies, waits for them, and re-layouts  2.02 us

profile of v4, /device:TPU:0, one launch (start us, length us, event | category | flops | bytes accessed | tf_op | source)
XLA Modules:
  0.0 64.7 jit_solution(15893692973762444222)
XLA Ops:
  0.0 62.7 %shard_map.64 = bf16[32,128,512]{2,1,0:T(8,128)(2,1)S(1)} custom-call(s32[1,32]{1,0:T(1,128)} %bitcast.1, f32[6,32,256]{2,1,0:T(8,128)} %angles_hbm.1, bf16[32,64,512]{2,1,0:T(8,128)(2,1)} %src_hbm.1, bf16[512,512]{1,0:T(8,128)(2,1)} %proj_hbm.1, bf16[5,2,512,512]{3,2,1,0:T(8,128)(2,1)} %w_hbm.1, bf16[256,1024]{1,0:T(8,128)(2,1)} %interp_hbm.1), custom_call_target="tpu_custom_call" | custom-call | tf_op jit(solution)/shard_map/pallas_call | solution.py:427
  62.7 2.0 %copy.8 = bf16[32,128,512]{2,1,0:T(8,128)(2,1)} copy(bf16[32,128,512]{2,1,0:T(8,128)(2,1)S(1)} %shard_map.64) | data formatting | bytes 8388608
